TPU v7x, 32 devices: a whole 2x2x4 slice. The times are simulated.
32 devices in a mesh: dp: 2 (over x), seq: 16 (over z, y, core).
Axes of the slice: x: 2, y: 2, z: 4, core: 2. Of those that a mesh axis runs over, the one named last changes fastest.
Arguments:
- tiles: bfloat16 [2, 16, 32, 4, 1024], P('dp', None, 'seq'), may hold values from -6 to 6
- patch_index: int32 [2, 16, 32, 4], P('dp', None, 'seq'), may hold values from 0 to 127
- pos_table: bfloat16 [128, 1024], replicated, may hold values from -6 to 6
- depth_kernel: bfloat16 [2, 27, 1024], replicated, may hold values from -1.25 to 1.25
- enc_gain: bfloat16 [2, 1024], replicated, may hold values from 0.099609375 to 1.8984375
- point_weight: bfloat16 [2, 1024, 1024], replicated, may hold values from -0.1875 to 0.1875
- action_ids: int32 [2, 16], replicated, may hold values from 0 to 7
- w_in: bfloat16 [1024, 5120], P('seq', 'dp'), may hold values from -0.1875 to 0.1875
- action_table: bfloat16 [8, 5120], P(None, 'dp'), may hold values from -6 to 6
- dyn_gain: bfloat16 [5120], P('dp'), may hold values from 0.099609375 to 1.8984375
- w_query: bfloat16 [5120, 5120], P('seq', 'dp'), may hold values from -0.078125 to 0.078125
- w_keyval: bfloat16 [5120, 2, 1024], P('seq', None, 'dp'), may hold values from -0.078125 to 0.078125
- seq_order: int32 [4], replicated, may hold values from 0 to 3, each once
Outputs:
- attended: bfloat16 [2, 16, 32, 4, 5120], P(None, None, 'seq', None, 'dp')
Inputs may be any that keep to these rules, and one draw needn't show every extreme that they name: `seq_order`: each of 0 to 3 appears once.
All inputs are finite; a program needn't handle non-finite values.
Results may differ from a plain program's by a relative error of at most 0.012.
Values may be sent and summed in bfloat16 or wider, within the bound.
A program may use at most 128 MiB of HBM per device.

v0:
```python
import jax
import jax.numpy as jnp
from jax import lax
from jax.sharding import PartitionSpec as P

DIM = 5120
HEAD = 128
Q_HEADS = 40
KV_HEADS = 8


def extended(block, sides, width):
    for axis, dim in sides:
        count = lax.axis_size(axis)
        forward = [(i, i + 1) for i in range(count - 1)]
        backward = [(target, source) for source, target in forward]
        low = lax.ppermute(
            lax.slice_in_dim(block, block.shape[dim] - width, None, axis=dim), axis, forward
        )
        high = lax.ppermute(lax.slice_in_dim(block, 0, width, axis=dim), axis, backward)
        block = jnp.concatenate([low, block, high], axis=dim)
    return block


def depth_block(padded, kernel, gains, weight):
    frames = padded.shape[1]
    height = padded.shape[2] - 2
    breadth = padded.shape[3]
    channels = padded.shape[4]
    framed = jnp.pad(padded.astype(jnp.float32), ((0, 0), (2, 0), (0, 0), (1, 1), (0, 0)))
    summed = jnp.zeros((padded.shape[0], frames, height, breadth, channels), jnp.float32)
    for time_tap in range(3):
        for row_tap in range(3):
            for col_tap in range(3):
                window = framed[
                    :,
                    time_tap : time_tap + frames,
                    row_tap : row_tap + height,
                    col_tap : col_tap + breadth,
                    :,
                ]
                summed = summed + window * kernel[9 * time_tap + 3 * row_tap + col_tap].astype(
                    jnp.float32
                )
    factor = lax.rsqrt(jnp.mean(summed * summed, axis=-1, keepdims=True) + 1e-05)
    normed = (summed * factor * gains.astype(jnp.float32)).astype(jnp.bfloat16)
    projected = jnp.dot(
        normed.reshape(-1, channels), weight, preferred_element_type=jnp.float32
    ).reshape(summed.shape)
    centre = padded[:, :, 1:-1].astype(jnp.float32)
    return (centre + jax.nn.gelu(projected)).astype(jnp.bfloat16)


def body(
    tiles,
    patch_index,
    pos_table,
    depth_kernel,
    enc_gain,
    point_weight,
    action_ids,
    w_in,
    action_table,
    dyn_gain,
    w_query,
    w_keyval,
    seq_order,
):
    frames = tiles.shape[1]
    height = tiles.shape[2]
    breadth = tiles.shape[3]
    channels = tiles.shape[4]
    positions = pos_table.shape[0]
    blocks = depth_kernel.shape[0]
    flat_index = patch_index.reshape(-1)
    position_pick = (flat_index[:, None] == jnp.arange(positions, dtype=jnp.int32)[None, :]).astype(
        jnp.bfloat16
    )
    placed = jnp.dot(position_pick, pos_table, preferred_element_type=jnp.float32).reshape(
        tiles.shape
    )
    hidden = (tiles.astype(jnp.float32) + placed).astype(jnp.bfloat16)
    for block_idx in range(blocks):
        padded = extended(hidden, (("seq", 2),), 1)
        hidden = depth_block(
            padded, depth_kernel[block_idx], enc_gain[block_idx], point_weight[block_idx]
        )
    latent = hidden.reshape(-1, channels)
    clips = action_ids.shape[0]
    actions = action_table.shape[0]
    cells = height * breadth
    action_range = jnp.arange(actions, dtype=jnp.int32)
    gathered = lax.all_gather(latent, "dp", axis=0, tiled=True)
    w_slab = lax.all_gather(w_in, "seq", axis=0, tiled=True)
    action_pick = (action_ids.reshape(-1)[:, None] == action_range[None, :]).astype(jnp.bfloat16)
    action_rows = jnp.dot(action_pick, action_table, preferred_element_type=jnp.float32)
    embed = jnp.dot(gathered, w_slab, preferred_element_type=jnp.float32).reshape(
        clips * frames, cells, -1
    )
    embed = jax.nn.gelu(embed + action_rows[:, None, :])
    squares = lax.psum(jnp.sum(embed * embed, axis=-1), "dp")
    factor = lax.rsqrt(squares / DIM + 1e-05)[:, :, None]
    normed = (
        (embed * factor * dyn_gain.astype(jnp.float32))
        .astype(jnp.bfloat16)
        .reshape(clips * frames * cells, -1)
    )
    inputs = lax.all_gather(normed, "dp", axis=1, tiled=True)
    pieces = (
        lax.all_gather(w_query, "seq", axis=0, tiled=True),
        lax.all_gather(w_keyval, "seq", axis=0, tiled=True),
    )
    span_rows = pieces[0].shape[0]
    query_sum = jnp.dot(inputs, pieces[0], preferred_element_type=jnp.float32)
    pair_sum = jnp.dot(inputs, pieces[1].reshape(span_rows, -1), preferred_element_type=jnp.float32)
    kv_local = w_keyval.shape[2] // HEAD
    group = Q_HEADS // KV_HEADS
    query_heads = query_sum.reshape(clips, frames, cells, kv_local, group, HEAD)
    pairs = pair_sum.reshape(clips, frames, cells, 2, kv_local, HEAD)
    key_heads = pairs[:, :, :, 0]
    value_heads = pairs[:, :, :, 1].astype(jnp.bfloat16)
    query_unit = query_heads * lax.rsqrt(
        jnp.mean(query_heads * query_heads, axis=-1, keepdims=True) + 1e-06
    )
    key_unit = key_heads * lax.rsqrt(
        jnp.mean(key_heads * key_heads, axis=-1, keepdims=True) + 1e-06
    )
    scores = jnp.einsum(
        "cfpkgh,ctpkh->cpkgft", query_unit, key_unit, precision=lax.Precision.HIGHEST
    ) * HEAD ** (-0.5)
    causal = (
        jnp.arange(frames, dtype=jnp.int32)[:, None] >= jnp.arange(frames, dtype=jnp.int32)[None, :]
    )
    raised = jnp.where(causal, jnp.exp(scores), 0.0)
    shares = (raised / jnp.sum(raised, axis=-1, keepdims=True)).astype(jnp.bfloat16)
    mixed = jnp.einsum(
        "cpkgft,ctpkh->cfpkgh", shares, value_heads, preferred_element_type=jnp.float32
    ).astype(jnp.bfloat16)
    mixed = mixed.reshape(clips, frames, height, breadth, -1)
    return jnp.take(mixed, seq_order, axis=3)


def solution(mesh):
    placed = (
        P("dp", None, "seq", None, None),
        P("dp", None, "seq", None),
        P(),
        P(),
        P(),
        P(),
        P(),
        P("seq", "dp"),
        P(None, "dp"),
        P("dp"),
        P("seq", "dp"),
        P("seq", None, "dp"),
        P(),
    )
    return jax.shard_map(
        body,
        mesh=mesh,
        in_specs=placed,
        out_specs=P(None, None, "seq", None, "dp"),
        check_vma=False,
    )
```

profile of v0, /device:TPU:0, one launch (start us, length us, event | category | flops | bytes accessed | tf_op | source)
XLA Modules:
  0.0 375.4 jit_solution(16638443497301449434)
XLA Ops:
  6.6 0.7 all-gather.5.cloned.1.call-update
  7.3 0.7 all-gather.9.cloned.1.call-update
  8.1 0.8 copy.46
  8.9 0.1 eq.30
  9.0 0.3 fusion.139
  9.3 0.1 reshape.919
  9.4 0.2 add_convert_fusion
  9.6 0.1 fusion.148
  9.7 1.3 collective-permute-start.1
  11.0 3.0 collective-permute-start
  14.1 0.1 eq.34
  14.2 0.1 slice_convert_fusion.27
  14.3 1.0 fusion.141
  15.3 0.3 maximum_convert_fusion
  15.6 4.4 %multiply_reduce_fusion.4 = (f32[16,2,4]{2,1,0:T(2,128)S(1)}, f32[1,16,2,4,1024]{4,3,2,1,0:T(4,128)S(1)}) fusion(f32[1024]{0:T(1024)S(1)} %bitcast.139, f32[1024]{0:T(1024)S(1)} %bitcast.140, f32[1,16,4,4,1024]{4,3,2,1,0:T(4,128)S(1)} %maximum_convert_fusion, f32[1024]{0:T(1024)S(1)} %bitcast.141, f32[1024]{0:T(1024)S(1)} %bitcast.142, ...), kind=kLoop, calls=%fused_computation.212 | loop fusion | flops 7208832 | bytes 3256832 | tf_op jit(solution)/shard_map/reduce_sum | solution.py:45
  20.1 0.1 copy.47
  20.2 0.1 copy.48
  20.3 0.2 multiply_convert_fusion.2
  20.5 0.1 reshape.920
  20.6 2.1 fusion.12
  22.7 0.1 reshape.921
  22.9 0.4 fusion.136
  23.3 0.1 fusion.147
  23.4 1.3 collective-permute-start.3
  24.7 6.1 %collective-permute-start.2 = (bf16[1,16,1,4,1024]{4,3,2,1,0:T(4,128)(2,1)S(1)}, bf16[1,16,1,4,1024]{4,3,2,1,0:T(4,128)(2,1)S(1)}, u32[]{:S(2)}, u32[]{:S(2)}) collective-permute-start(bf16[1,16,1,4,1024]{4,3,2,1,0:T(4,128)(2,1)S(1)} %get-tuple-element.9), channel_id=1, source_target_pairs={{0,1},{1,2},{2,3},{3,4},{4,5},{5,6},{6,7},{7,8},{8,9},{9,10},{10,1... | collective-permute-start | bytes 393224 | tf_op jit(solution)/shard_map/ppermute | solution.py:17
  30.8 0.1 slice_convert_fusion.28
  30.9 0.9 collective-permute-done.2
  31.8 0.3 maximum_convert_fusion.1
  32.1 4.4 %multiply_reduce_fusion.3 = (f32[16,2,4]{2,1,0:T(2,128)S(1)}, f32[1,16,2,4,1024]{4,3,2,1,0:T(4,128)S(1)}) fusion(f32[1024]{0:T(1024)S(1)} %bitcast.117, f32[1024]{0:T(1024)S(1)} %bitcast.118, f32[1,16,4,4,1024]{4,3,2,1,0:T(4,128)S(1)} %maximum_convert_fusion.1, f32[1024]{0:T(1024)S(1)} %bitcast.153, f32[1024]{0:T(1024)S(1)} %bitcast.154, ...), kind=kLoop, calls=%fused_computation.210 | loop fusion | flops 7208832 | bytes 3256832 | tf_op jit(solution)/shard_map/reduce_sum | solution.py:45
  36.5 0.1 copy.49
  36.6 0.1 copy.50
  36.7 0.2 multiply_convert_fusion.1
  36.9 0.1 reshape.922
  37.0 2.1 fusion.10
  39.1 0.1 reshape.923
  39.2 0.4 fusion.135
  39.6 0.1 reshape.924
  39.7 7.0 %all_gather.15 = bf16[256,1024]{1,0:T(8,128)(2,1)S(1)} all-gather(bf16[128,1024]{1,0:T(8,128)(2,1)S(1)} %reshape.924), channel_id=1, replica_groups=mesh['dp'=2,'seq'=16] {'dp'}, dimensions={0}, use_global_device_ids=true | all-gather | bytes 786432 | tf_op jit(solution)/shard_map/all_gather | solution.py:93
  46.8 21.4 %all-gather.5.cloned.1.call-done = bf16[1024,2560]{1,0:T(8,128)(2,1)} async-done(((bf16[64,2560]{1,0:T(8,128)(2,1)}), bf16[1024,2560]{1,0:T(8,128)(2,1)}) %all-gather.5.cloned.1.call-update) | async-done | bytes 5242896 | tf_op jit(solution)/shard_map/all_gather | solution.py:94
  68.2 4.6 %multiply_reduce_fusion.1 = (f32[256]{0:T(256)S(1)}, f32[256,2560]{1,0:T(8,128)S(1)}) fusion(f32[32,2560]{1,0:T(8,128)} %fusion.141, bf16[256,1024]{1,0:T(8,128)(2,1)S(1)} %all_gather.15, bf16[1024,2560]{1,0:T(8,128)(2,1)} %all-gather.5.cloned.1.call-done), kind=kOutput, calls=%fused_computation.64 | convolution fusion | flops 1349385984 | bytes 8717312 | tf_op jit(solution)/shard_map/dot_general | solution.py:97
  72.8 0.1 reduce_sum.59
  72.8 8.1 %psum.7 = f32[32,8]{1,0:T(8,128)S(1)} all-reduce(f32[32,8]{1,0:T(8,128)S(1)} %reduce_sum.59), channel_id=1, replica_groups=mesh['dp'=2,'seq'=16] {'dp'}, use_global_device_ids=true, to_apply=%region_3.4 | all-reduce | flops 256 | bytes 2048 | tf_op jit(solution)/shard_map/psum | solution.py:101
  81.0 0.1 mul.774
  81.1 1.3 multiply_convert_fusion
  82.4 0.2 all-gather.11.cloned.1.call-start
  82.7 0.3 all-gather.11.cloned.1.call-update
  83.1 73.5 %all-gather.9.cloned.1.call-done = bf16[5120,2,512]{2,1,0:T(2,128)(2,1)} async-done(((bf16[320,2,512]{2,1,0:T(2,128)(2,1)}), bf16[5120,2,512]{2,1,0:T(2,128)(2,1)}) %all-gather.9.cloned.1.call-update) | async-done | bytes 10485776 | tf_op jit(solution)/shard_map/all_gather | solution.py:111
  156.6 26.3 %copy.63 = bf16[5120,2,512]{0,2,1:T(8,128)(2,1)} copy(bf16[5120,2,512]{2,1,0:T(2,128)(2,1)} %all-gather.9.cloned.1.call-done) | data formatting | bytes 20971520 | tf_op jit(solution)/shard_map/reshape | solution.py:115
  182.9 12.5 %all-gather.7.cloned.1.call-done = bf16[256,5120]{1,0:T(8,128)(2,1)} async-done(((bf16[256,2560]{1,0:T(8,128)(2,1)}), bf16[256,5120]{1,0:T(8,128)(2,1)}) %all-gather.7.cloned.1.call-update) | async-done | bytes 2621456 | tf_op jit(solution)/shard_map/all_gather | solution.py:108
  195.4 6.5 %fusion.149 = f32[2,16,8,2,4,128]{5,2,4,3,1,0:T(8,128)S(1)} fusion(bf16[2,16,8,5120,1,1]{3,2,5,4,1,0:T(8,128)(2,1)} %bitcast.173, bf16[2,4,128,5120,1,1]{3,2,1,0,5,4:T(8,128)(2,1)} %bitcast.114), kind=kOutput, calls=%fused_computation.292 | convolution fusion | flops 2684354560 | bytes 14155776 | tf_op jit(solution)/shard_map/dot_general | solution.py:115
  201.9 0.3 multiply_reduce_fusion.2
  202.2 0.2 multiply_bitcast_fusion
  202.4 127.9 %all-gather.11.cloned.1.call-done = bf16[5120,2560]{1,0:T(8,128)(2,1)} async-done(((bf16[320,2560]{1,0:T(8,128)(2,1)}), bf16[5120,2560]{1,0:T(8,128)(2,1)}) %all-gather.11.cloned.1.call-update) | async-done | bytes 26214416 | tf_op jit(solution)/shard_map/all_gather | solution.py:110
  330.4 12.8 %fusion.150 = f32[256,2560]{1,0:T(8,128)S(1)} fusion(bf16[256,5120]{1,0:T(8,128)(2,1)} %all-gather.7.cloned.1.call-done, bf16[5120,2560]{1,0:T(8,128)(2,1)} %all-gather.11.cloned.1.call-done), kind=kOutput, calls=%fused_computation.293 | convolution fusion | flops 6710886400 | bytes 31457280 | tf_op jit(solution)/shard_map/dot_general | solution.py:114
  343.1 0.7 multiply_reduce_fusion
  343.9 0.1 add_rsqrt_fusion
  344.0 0.8 broadcast_multiply_fusion
  344.8 15.7 %fusion.9 = (f32[2,8,4,5,16]{4,3,2,1,0:T(8,128)S(1)}, f32[2,8,4,16,16,5]{4,3,5,2,1,0:T(8,128)S(1)}) fusion(pred[16,16]{0,1:T(8,128)(4,1)S(1)} %iota_compare_fusion.4, f32[2,16,8,4,5,128]{5,2,4,3,1,0:T(8,128)S(1)} %broadcast_multiply_fusion, f32[2,16,8,4,128,1]{4,2,3,1,0,5:T(8,128)S(1)} %multiply_bitcast_fusion), kind=kOutput, calls=%fused_computation.65 | convolution fusion | flops 126069760 | bytes 3494144 | tf_op jit(solution)/shard_map/cfpkgh,ctpkh->cpkgft/dot_general | solution.py:128
  360.5 1.2 fusion.16
  361.7 0.5 copy.56
  362.3 2.3 reshape.927
  364.6 2.0 gather_fusion
  366.6 0.2 select_bitcast_fusion
  366.8 2.1 copy.57
  (37 shorter events, 0.4 us)
Async XLA Ops:
  6.5 2.5 copy-start
  6.5 2.9 copy-start.3
  6.5 7.5 %copy-start.7 = (s32[2,16]{1,0:T(2,128)S(1)}, s32[2,16]{1,0:T(2,128)}, u32[]{:S(2)}) copy-start(s32[2,16]{1,0:T(2,128)} %param.19) | copy-start | bytes 388
  6.5 7.6 %copy-start.6 = (bf16[2560]{0:T(1024)(128)(2,1)S(1)}, bf16[2560]{0:T(1024)(128)(2,1)}, u32[]{:S(2)}) copy-start(bf16[2560]{0:T(1024)(128)(2,1)} %param.22) | copy-start | bytes 15364
  6.5 7.6 %copy-start.2 = (bf16[2,27,1024]{2,0,1:T(2,128)(2,1)S(1)}, bf16[2,27,1024]{2,0,1:T(2,128)(2,1)}, u32[]{:S(2)}) copy-start(bf16[2,27,1024]{2,0,1:T(2,128)(2,1)} %param.16) | copy-start | bytes 331780
  6.5 7.7 %copy-start.4 = (bf16[8,2560]{1,0:T(8,128)(2,1)S(1)}, bf16[8,2560]{1,0:T(8,128)(2,1)}, u32[]{:S(2)}) copy-start(bf16[8,2560]{1,0:T(8,128)(2,1)} %param.21) | copy-start | bytes 122884
  6.6 8.7 %copy-start.5 = (bf16[2,1024]{1,0:T(2,128)(2,1)S(1)}, bf16[2,1024]{1,0:T(2,128)(2,1)}, u32[]{:S(2)}) copy-start(bf16[2,1024]{1,0:T(2,128)(2,1)} %param.17) | copy-start | bytes 12292
  6.6 61.6 %all-gather.5.cloned.1.call-start = ((), (), s32[]{:S(2)}) async-start(), calls=%async_computation | async-start | bytes 5570560 | tf_op jit(solution)/shard_map/all_gather | solution.py:94
  7.3 149.3 %all-gather.9.cloned.1.call-start = ((), (), s32[]{:S(2)}) async-start(), calls=%async_computation.2 | async-start | bytes 11141120 | tf_op jit(solution)/shard_map/all_gather | solution.py:111
  8.1 187.4 %all-gather.7.cloned.1.call-start = ((), (), s32[]{:S(2)}) async-start(), calls=%async_computation.1 | async-start | bytes 3932160 | tf_op jit(solution)/shard_map/all_gather | solution.py:108
  9.7 5.6 %collective-permute-start.1 = (bf16[1,16,1,4,1024]{4,3,2,1,0:T(4,128)(2,1)S(1)}, bf16[1,16,1,4,1024]{4,3,2,1,0:T(4,128)(2,1)S(1)}, u32[]{:S(2)}, u32[]{:S(2)}) collective-permute-start(bf16[1,16,1,4,1024]{4,3,2,1,0:T(4,128)(2,1)S(1)} %get-tuple-element.12), channel_id=1, source_target_pairs={{1,0},{2,1},{3,2},{4,3},{5,4},{6,5},{7,6},{8,7},{9,8},{10,9},{11,1... | collective-permute-start | bytes 393224 | tf_op jit(solution)/shard_map/ppermute | solution.py:20
  11.0 4.3 %collective-permute-start = (bf16[1,16,1,4,1024]{4,3,2,1,0:T(4,128)(2,1)S(1)}, bf16[1,16,1,4,1024]{4,3,2,1,0:T(4,128)(2,1)S(1)}, u32[]{:S(2)}, u32[]{:S(2)}) collective-permute-start(bf16[1,16,1,4,1024]{4,3,2,1,0:T(4,128)(2,1)S(1)} %get-tuple-element.11), channel_id=1, source_target_pairs={{0,1},{1,2},{2,3},{3,4},{4,5},{5,6},{6,7},{7,8},{8,9},{9,10},{10,1... | collective-permute-start | bytes 393224 | tf_op jit(solution)/shard_map/ppermute | solution.py:17
  23.4 7.5 %collective-permute-start.3 = (bf16[1,16,1,4,1024]{4,3,2,1,0:T(4,128)(2,1)S(1)}, bf16[1,16,1,4,1024]{4,3,2,1,0:T(4,128)(2,1)S(1)}, u32[]{:S(2)}, u32[]{:S(2)}) collective-permute-start(bf16[1,16,1,4,1024]{4,3,2,1,0:T(4,128)(2,1)S(1)} %get-tuple-element.10), channel_id=1, source_target_pairs={{1,0},{2,1},{3,2},{4,3},{5,4},{6,5},{7,6},{8,7},{9,8},{10,9},{11,1... | collective-permute-start | bytes 393224 | tf_op jit(solution)/shard_map/ppermute | solution.py:20
  24.7 7.1 %collective-permute-start.2 = (bf16[1,16,1,4,1024]{4,3,2,1,0:T(4,128)(2,1)S(1)}, bf16[1,16,1,4,1024]{4,3,2,1,0:T(4,128)(2,1)S(1)}, u32[]{:S(2)}, u32[]{:S(2)}) collective-permute-start(bf16[1,16,1,4,1024]{4,3,2,1,0:T(4,128)(2,1)S(1)} %get-tuple-element.9), channel_id=1, source_target_pairs={{0,1},{1,2},{2,3},{3,4},{4,5},{5,6},{6,7},{7,8},{8,9},{9,10},{10,1... | collective-permute-start | bytes 393224 | tf_op jit(solution)/shard_map/ppermute | solution.py:17
  81.1 2.0 copy-start.8
  82.4 247.9 %all-gather.11.cloned.1.call-start = ((), (), s32[]{:S(2)}) async-start(), calls=%async_computation.3 | async-start | bytes 27852800 | tf_op jit(solution)/shard_map/all_gather | solution.py:110
  364.6 4.3 %copy-start.1 = (bf16[128,1024]{1,0:T(8,128)(2,1)S(1)}, bf16[128,1024]{1,0:T(8,128)(2,1)}, u32[]{:S(2)}) copy-start(bf16[128,1024]{1,0:T(8,128)(2,1)} %param.15) | copy-start | bytes 786436
Sparse Core Ops, SparseCore 0:
  9.7 58.4 all-gather.4
  70.4 86.0 all-gather.8
  158.1 37.2 all-gather.6
  196.9 133.4 all-gather.10
where the time goes:
time: 376 us; the launch traced here: 375 us
  waiting for transfers between devices  238 us (63%)
  matrix products  46.1 us (12%)
  local copies, waits for them, and re-layouts  35.7 us (9%)
  blocking collectives  15.2 us (4%)
  other arithmetic  14.9 us (4%)
  between operations  13.5 us (4%)
  starting transfers between devices  12.1 us (3%)
    all_gather x1, waiting for transfers between devices, body(): lax.all_gather(w_query, 'seq', axis=0, tiled=True)  128 us
    all_gather x1, waiting for transfers between devices, body(): lax.all_gather(w_keyval, 'seq', axis=0, tiled=True)  73.5 us
    reshape x1, local copies, waits for them, and re-layouts, body(): pieces[1].reshape(span_rows, -1)  26.3 us
    all_gather x1, waiting for transfers between devices, body(): w_slab = lax.all_gather(w_in, 'seq', axis=0, tiled=True)  21.4 us
    dot_general x1, matrix products, body(): jnp.einsum('cfpkgh,ctpkh->cpkgft', query_unit, key_unit, precision=lax.Pr...  15.7 us
    dot_general x1, matrix products, body(): query_sum = jnp.dot(inputs, pieces[0], preferred_element_type=jnp.float32)  12.8 us
    all_gather x1, waiting for transfers between devices, body(): inputs = lax.all_gather(normed, 'dp', axis=1, tiled=True)  12.5 us
    ppermute x2, starting transfers between devices, extended(): lax.ppermute(lax.slice_in_dim(block, block.shape[dim] - width, None, axis...  9.14 us
  transfers between devices with their start and end apart: 8, of which 5 were waited for; matrix products, arithmetic and copies ran while one was open for 16% of the time, Pallas kernels for 0%

commit v1 on v0

--- a/solution.py
+++ b/solution.py
@@ -108,7 +108,9 @@
     inputs = lax.all_gather(normed, "dp", axis=1, tiled=True)
     pieces = (
         lax.all_gather(w_query, "seq", axis=0, tiled=True),
-        lax.all_gather(w_keyval, "seq", axis=0, tiled=True),
+        jnp.concatenate(
+            lax.all_to_all(jnp.stack([w_keyval] * lax.axis_size("seq")), "seq", 0, 0), axis=0
+        ),
     )
     span_rows = pieces[0].shape[0]
     query_sum = jnp.dot(inputs, pieces[0], preferred_element_type=jnp.float32)

time: 376 us -> 523 us (1.39)
  the two profiles are of different devices: /device:TPU:0 before, /device:TPU:13 now
where the time goes in v1:
time: 523 us; the launch traced here: 514 us
  waiting for transfers between devices  358 us (68%)
  matrix products  46 us (9%)
  local copies, waits for them, and re-layouts  43.9 us (8%)
  starting transfers between devices  22.3 us (4%)
  other arithmetic  16.1 us (3%)
  between operations  13.7 us (3%)
  blocking collectives  13.5 us (3%)
    all_to_all x1, waiting for transfers between devices, body(): lax.all_to_all(jnp.stack([w_keyval] * lax.axis_size('seq')), 'seq', 0, 0)  339 us
    dot_general x1, matrix products, body(): jnp.einsum('cfpkgh,ctpkh->cpkgft', query_unit, key_unit, precision=lax.Pr...  15.7 us
    all_gather x1, waiting for transfers between devices, body(): w_slab = lax.all_gather(w_in, 'seq', axis=0, tiled=True)  15.3 us
    dot_general x1, local copies, waits for them, and re-layouts, body(): jnp.dot(inputs, pieces[1].reshape(span_rows, -1), preferred_element_type=...  13.9 us
    dot_general x1, matrix products, body(): query_sum = jnp.dot(inputs, pieces[0], preferred_element_type=jnp.float32)  12.8 us
    unnamed x20, local copies, waits for them, and re-layouts  12.2 us
  transfers between devices with their start and end apart: 8, of which 5 were waited for; matrix products, arithmetic and copies ran while one was open for 12% of the time, Pallas kernels for 0%

profile of v1, /device:TPU:13, one launch (start us, length us, event | category | flops | bytes accessed | tf_op | source)
XLA Modules:
  0.0 513.6 jit_solution(1115510435195503946)
XLA Ops:
  6.6 0.7 all-gather.4.cloned.1.call-update
  7.3 0.8 copy.46
  8.1 0.1 eq.30
  8.2 0.3 fusion.139
  8.5 0.1 reshape.918
  8.7 1.1 add_convert_fusion
  9.8 0.1 fusion.148
  9.9 2.6 collective-permute-start.1
  12.5 3.9 collective-permute-start
  16.4 0.1 eq.34
  16.5 0.1 slice_convert_fusion.27
  16.6 1.0 fusion.141
  17.6 0.7 collective-permute-done
  18.3 0.3 maximum_convert_fusion
  18.6 4.4 multiply_reduce_fusion.4
  23.1 0.1 copy.47
  23.2 0.1 copy.48
  23.3 0.2 multiply_convert_fusion.2
  23.5 2.0 fusion.12
  25.6 0.1 reshape.920
  25.7 0.4 fusion.136
  26.2 0.1 fusion.147
  26.3 2.8 collective-permute-start.3
  29.1 4.4 collective-permute-start.2
  33.5 0.1 slice_convert_fusion.28
  33.5 1.1 collective-permute-done.3
  34.6 0.7 collective-permute-done.2
  35.4 0.3 maximum_convert_fusion.1
  35.7 4.4 multiply_reduce_fusion.3
  40.2 0.1 copy.49
  40.3 0.1 copy.50
  40.4 0.2 multiply_convert_fusion.1
  40.6 0.1 reshape.921
  40.6 2.0 fusion.10
  42.7 0.1 reshape.922
  42.8 0.4 fusion.135
  43.3 7.4 %all_gather.12 = bf16[256,1024]{1,0:T(8,128)(2,1)S(1)} all-gather(bf16[128,1024]{1,0:T(8,128)(2,1)S(1)} %reshape.923), channel_id=1, replica_groups=mesh['dp'=2,'seq'=16] {'dp'}, dimensions={0}, use_global_device_ids=true | all-gather | bytes 786432 | tf_op jit(solution)/shard_map/all_gather | solution.py:93
  50.7 15.3 %all-gather.4.cloned.1.call-done = bf16[1024,2560]{1,0:T(8,128)(2,1)} async-done(((bf16[64,2560]{1,0:T(8,128)(2,1)}), bf16[1024,2560]{1,0:T(8,128)(2,1)}) %all-gather.4.cloned.1.call-update) | async-done | bytes 5242896 | tf_op jit(solution)/shard_map/all_gather | solution.py:94
  66.0 4.6 multiply_reduce_fusion.1
  70.6 0.1 reduce_sum.59
  70.7 6.1 %psum.7 = f32[32,8]{1,0:T(8,128)S(1)} all-reduce(f32[32,8]{1,0:T(8,128)S(1)} %reduce_sum.59), channel_id=1, replica_groups=mesh['dp'=2,'seq'=16] {'dp'}, use_global_device_ids=true, to_apply=%region_3.4 | all-reduce | flops 256 | bytes 2048 | tf_op jit(solution)/shard_map/psum | solution.py:101
  76.8 0.1 mul.774
  77.0 1.3 multiply_convert_fusion
  78.3 0.5 all-gather.8.cloned.1.call-start
  78.8 0.2 all-gather.8.cloned.1.call-update
  79.1 9.3 %stack.2 = bf16[16,320,2,512]{3,2,1,0:T(2,128)(2,1)} broadcast(bf16[320,2,512]{2,1,0:T(2,128)(2,1)S(1)} %copy-done.2), dimensions={1,2,3} | broadcast | bytes 11141120 | tf_op jit(solution)/shard_map/stack | solution.py:112
  88.4 8.0 %all-to-all-start = ((bf16[16,320,2,512]{3,2,1,0:T(2,128)(2,1)}), bf16[16,320,2,512]{3,2,1,0:T(2,128)(2,1)}, u32[]{:S(2)}, u32[]{:S(2)}) async-start(bf16[16,320,2,512]{3,2,1,0:T(2,128)(2,1)} %stack.2), calls=%async_computation | async-start | bytes 20971520 | tf_op jit(solution)/shard_map/all_to_all | solution.py:112
  96.5 339.4 %all-to-all-done = bf16[16,320,2,512]{3,2,1,0:T(2,128)(2,1)} async-done(((bf16[16,320,2,512]{3,2,1,0:T(2,128)(2,1)}), bf16[16,320,2,512]{3,2,1,0:T(2,128)(2,1)}, u32[]{:S(2)}, u32[]{:S(2)}) %all-to-all-start) | async-done | bytes 10485792 | tf_op jit(solution)/shard_map/all_to_all | solution.py:112
  435.8 11.4 %copy.67 = bf16[640,8,2,512]{3,1,2,0:T(8,128)(2,1)} copy(bf16[640,8,2,512]{3,2,1,0:T(2,128)(2,1)} %bitcast.80) | data formatting | bytes 20971520
  447.2 13.9 %copy.51 = bf16[1024,5120]{1,0:T(8,128)(2,1)} copy(bf16[1024,5120]{0,1:T(8,128)(2,1)} %bitcast.115) | data formatting | bytes 20971520 | tf_op jit(solution)/shard_map/dot_general | solution.py:117
  461.1 6.5 %fusion.149 = f32[2,16,8,2,4,128]{5,2,4,3,1,0:T(8,128)S(1)} fusion(bf16[2,16,8,5120,1,1]{3,2,5,4,1,0:T(8,128)(2,1)} %bitcast.175, bf16[2,4,128,5120,1,1]{3,2,1,0,5,4:T(8,128)(2,1)} %bitcast.116), kind=kOutput, calls=%fused_computation.292 | convolution fusion | flops 2684354560 | bytes 14155776 | tf_op jit(solution)/shard_map/dot_general | solution.py:117
  467.6 0.3 multiply_reduce_fusion.2
  467.9 0.2 multiply_bitcast_fusion
  468.1 12.8 %fusion.150 = f32[256,2560]{1,0:T(8,128)S(1)} fusion(bf16[256,5120]{1,0:T(8,128)(2,1)} %all-gather.6.cloned.1.call-done, bf16[5120,2560]{1,0:T(8,128)(2,1)} %all-gather.8.cloned.1.call-done), kind=kOutput, calls=%fused_computation.293 | convolution fusion | flops 6710886400 | bytes 31457280 | tf_op jit(solution)/shard_map/dot_general | solution.py:116
  480.9 0.7 multiply_reduce_fusion
  481.7 0.1 add_rsqrt_fusion
  481.8 1.1 broadcast_multiply_fusion
  482.8 15.7 %fusion.9 = (f32[2,8,4,5,16]{4,3,2,1,0:T(8,128)S(1)}, f32[2,8,4,16,16,5]{4,3,5,2,1,0:T(8,128)S(1)}) fusion(pred[16,16]{0,1:T(8,128)(4,1)S(1)} %iota_compare_fusion.4, f32[2,16,8,4,5,128]{5,2,4,3,1,0:T(8,128)S(1)} %broadcast_multiply_fusion, f32[2,16,8,4,128,1]{4,2,3,1,0,5:T(8,128)S(1)} %multiply_bitcast_fusion), kind=kOutput, calls=%fused_computation.65 | convolution fusion | flops 126069760 | bytes 3494144 | tf_op jit(solution)/shard_map/cfpkgh,ctpkh->cpkgft/dot_general | solution.py:130
  498.6 1.2 fusion.16
  499.7 0.5 copy.56
  500.3 2.3 reshape.925
  502.6 2.0 gather_fusion
  504.6 0.2 select_bitcast_fusion
  504.8 2.1 copy.57
  (38 shorter events, 0.5 us)
Async XLA Ops:
  6.5 1.7 copy-start
  6.5 9.8 %copy-start.7 = (s32[2,16]{1,0:T(2,128)S(1)}, s32[2,16]{1,0:T(2,128)}, u32[]{:S(2)}) copy-start(s32[2,16]{1,0:T(2,128)} %param.19) | copy-start | bytes 388
  6.5 9.9 %copy-start.6 = (bf16[2560]{0:T(1024)(128)(2,1)S(1)}, bf16[2560]{0:T(1024)(128)(2,1)}, u32[]{:S(2)}) copy-start(bf16[2560]{0:T(1024)(128)(2,1)} %param.22) | copy-start | bytes 15364
  6.5 9.9 %copy-start.3 = (bf16[2,27,1024]{2,0,1:T(2,128)(2,1)S(1)}, bf16[2,27,1024]{2,0,1:T(2,128)(2,1)}, u32[]{:S(2)}) copy-start(bf16[2,27,1024]{2,0,1:T(2,128)(2,1)} %param.16) | copy-start | bytes 331780
  6.5 10.1 %copy-start.4 = (bf16[8,2560]{1,0:T(8,128)(2,1)S(1)}, bf16[8,2560]{1,0:T(8,128)(2,1)}, u32[]{:S(2)}) copy-start(bf16[8,2560]{1,0:T(8,128)(2,1)} %param.21) | copy-start | bytes 122884
  6.5 11.0 %copy-start.5 = (bf16[2,1024]{1,0:T(2,128)(2,1)S(1)}, bf16[2,1024]{1,0:T(2,128)(2,1)}, u32[]{:S(2)}) copy-start(bf16[2,1024]{1,0:T(2,128)(2,1)} %param.17) | copy-start | bytes 12292
  6.6 59.5 %all-gather.4.cloned.1.call-start = ((), (), s32[]{:S(2)}) async-start(), calls=%async_computation.1 | async-start | bytes 5570560 | tf_op jit(solution)/shard_map/all_gather | solution.py:94
  7.3 453.8 %all-gather.6.cloned.1.call-start = ((), (), s32[]{:S(2)}) async-start(), calls=%async_computation.2 | async-start | bytes 3932160 | tf_op jit(solution)/shard_map/all_gather | solution.py:108
  9.9 7.7 %collective-permute-start.1 = (bf16[1,16,1,4,1024]{4,3,2,1,0:T(4,128)(2,1)S(1)}, bf16[1,16,1,4,1024]{4,3,2,1,0:T(4,128)(2,1)S(1)}, u32[]{:S(2)}, u32[]{:S(2)}) collective-permute-start(bf16[1,16,1,4,1024]{4,3,2,1,0:T(4,128)(2,1)S(1)} %get-tuple-element.12), channel_id=1, source_target_pairs={{1,0},{2,1},{3,2},{4,3},{5,4},{6,5},{7,6},{8,7},{9,8},{10,9},{11,1... | collective-permute-start | bytes 393224 | tf_op jit(solution)/shard_map/ppermute | solution.py:20
  12.5 5.8 %collective-permute-start = (bf16[1,16,1,4,1024]{4,3,2,1,0:T(4,128)(2,1)S(1)}, bf16[1,16,1,4,1024]{4,3,2,1,0:T(4,128)(2,1)S(1)}, u32[]{:S(2)}, u32[]{:S(2)}) collective-permute-start(bf16[1,16,1,4,1024]{4,3,2,1,0:T(4,128)(2,1)S(1)} %get-tuple-element.11), channel_id=1, source_target_pairs={{0,1},{1,2},{2,3},{3,4},{4,5},{5,6},{6,7},{7,8},{8,9},{9,10},{10,1... | collective-permute-start | bytes 393224 | tf_op jit(solution)/shard_map/ppermute | solution.py:17
  26.3 8.4 %collective-permute-start.3 = (bf16[1,16,1,4,1024]{4,3,2,1,0:T(4,128)(2,1)S(1)}, bf16[1,16,1,4,1024]{4,3,2,1,0:T(4,128)(2,1)S(1)}, u32[]{:S(2)}, u32[]{:S(2)}) collective-permute-start(bf16[1,16,1,4,1024]{4,3,2,1,0:T(4,128)(2,1)S(1)} %get-tuple-element.10), channel_id=1, source_target_pairs={{1,0},{2,1},{3,2},{4,3},{5,4},{6,5},{7,6},{8,7},{9,8},{10,9},{11,1... | collective-permute-start | bytes 393224 | tf_op jit(solution)/shard_map/ppermute | solution.py:20
  29.1 6.3 %collective-permute-start.2 = (bf16[1,16,1,4,1024]{4,3,2,1,0:T(4,128)(2,1)S(1)}, bf16[1,16,1,4,1024]{4,3,2,1,0:T(4,128)(2,1)S(1)}, u32[]{:S(2)}, u32[]{:S(2)}) collective-permute-start(bf16[1,16,1,4,1024]{4,3,2,1,0:T(4,128)(2,1)S(1)} %get-tuple-element.9), channel_id=1, source_target_pairs={{0,1},{1,2},{2,3},{3,4},{4,5},{5,6},{6,7},{7,8},{8,9},{9,10},{10,1... | collective-permute-start | bytes 393224 | tf_op jit(solution)/shard_map/ppermute | solution.py:17
  76.9 2.1 copy-start.2
  78.3 389.8 %all-gather.8.cloned.1.call-start = ((), (), s32[]{:S(2)}) async-start(), calls=%async_computation.3 | async-start | bytes 27852800 | tf_op jit(solution)/shard_map/all_gather | solution.py:110
  88.4 8.1 %copy-start.8 = (s32[4]{0:T(128)S(1)}, s32[4]{0:T(128)}, u32[]{:S(2)}) copy-start(s32[4]{0:T(128)} %param.25) | copy-start | bytes 52
  88.4 347.4 %all-to-all-start = ((bf16[16,320,2,512]{3,2,1,0:T(2,128)(2,1)}), bf16[16,320,2,512]{3,2,1,0:T(2,128)(2,1)}, u32[]{:S(2)}, u32[]{:S(2)}) async-start(bf16[16,320,2,512]{3,2,1,0:T(2,128)(2,1)} %stack.2), calls=%async_computation | async-start | bytes 20971520 | tf_op jit(solution)/shard_map/all_to_all | solution.py:112
  502.6 4.3 copy-start.1
Sparse Core Ops, SparseCore 0:
  9.6 56.3 all-gather.3
  78.4 39.0 all-gather.5
  119.1 329.4 all-gather.7
